TPU v7x, 32 devices: a whole 2x2x4 slice. The times are simulated.
32 devices in a mesh: groups: 2 (over x), head: 8 (over z, y), batch: 2 (over core).
Axes of the slice: x: 2, y: 2, z: 4, core: 2. Of those that a mesh axis runs over, the one named last changes fastest.
Arguments:
- latent_rows: bfloat16 [4096, 576], P(('groups', 'batch', 'head')), parts along dimension 0, may hold values from -6 to 6
- pre_queries: bfloat16 [4096, 128, 192], P(('groups', 'batch'), 'head'), parts along dimension 0, may hold values from -270 to 270
- pre_lengths: int32 [4, 4], P('groups'), parts along dimension 0, may hold values from 1 to 512, 1024 in all within a row
- owner_map: int32 [4, 4], P('groups'), parts along dimension 0, may hold values from 0 to 31, as said below
- context_cache: bfloat16 [64, 4096, 576], P(('groups', 'batch', 'head')), parts along dimension 0, may hold values from -6 to 6
- context_lengths: int32 [64], P(('groups', 'batch', 'head')), parts along dimension 0, may hold values from 1 to 4096, 65536 in all
- new_latent: bfloat16 [4, 32, 576], P('groups', ('batch', 'head')), parts along dimension 0, may hold values from -6 to 6
- dec_queries: bfloat16 [4, 32, 128, 192], P('groups', 'batch', 'head'), parts along dimension 0, may hold values from -270 to 270
- key_weight: bfloat16 [512, 16384], P(None, 'head'), may hold values from -0.25 to 0.25
- value_weight: bfloat16 [512, 16384], P(None, 'head'), may hold values from -0.25 to 0.25
Outputs:
- prefill_out: bfloat16 [4096, 16384], P(('groups', 'batch'), 'head'), parts along dimension 0
- decode_out: bfloat16 [4, 32, 16384], P('groups', 'batch', 'head'), parts along dimension 0
There are 2 independent parts, one for each index of `groups`. A program takes and returns all parts, laid end to end along the dimension named above; an argument that names none is the same for every part. Nothing has to cross between parts.
Inputs may be any that keep to these rules, and one draw needn't show every extreme that they name: `owner_map`: the entries are distinct decode requests.
All inputs are finite; a program needn't handle non-finite values. No bound on the sum of `context_lengths` on one device may be relied on, other than what follows from the above.
Results may differ from a plain program's by a relative error of at most 0.0061.
Values may be sent and summed in bfloat16 or wider, within the bound.
A program may use at most 192 MiB of HBM per device.

v0:
```python
import functools
import math

import jax
import jax.numpy as jnp
from jax import lax
from jax.experimental import pallas as pl
from jax.experimental.pallas import tpu as pltpu
from jax.sharding import PartitionSpec as P

BLK = 512


NEGATIVE = -1e30


def from_partner(value, axis, distance):
    mask = 2**distance
    pairs = [(source, source ^ mask) for source in range(lax.axis_size(axis))]
    return lax.ppermute(value, axis, pairs)


def request_table(pre_lengths, owner_map, span_len):
    seg_ends = jnp.cumsum(pre_lengths, axis=1)
    span_base = jnp.arange(pre_lengths.shape[0], dtype=jnp.int32)[:, None] * span_len
    seg_starts = seg_ends - pre_lengths + span_base
    return (owner_map.reshape(-1), seg_starts.reshape(-1), pre_lengths.reshape(-1))


def prefill_heads(own_span, queries, span_lengths, key_weight, value_weight):
    span_len, head_count, query_width = queries.shape
    head_size = key_weight.shape[1] // head_count
    lat_width = key_weight.shape[0]
    score_scale = 1.0 / math.sqrt(query_width)
    latent = own_span[:, :lat_width]
    rope_keys = own_span[:, lat_width:]
    keys_nope = (
        jnp.dot(latent, key_weight, preferred_element_type=jnp.float32)
        .astype(jnp.bfloat16)
        .reshape(span_len, head_count, head_size)
    )
    values = (
        jnp.dot(latent, value_weight, preferred_element_type=jnp.float32)
        .astype(jnp.bfloat16)
        .reshape(span_len, head_count, head_size)
    )
    scores = jnp.einsum(
        "qhd,khd->hqk", queries[:, :, :head_size], keys_nope, preferred_element_type=jnp.float32
    )
    scores = scores + jnp.einsum(
        "qhr,kr->hqk", queries[:, :, head_size:], rope_keys, preferred_element_type=jnp.float32
    )
    scores = scores * score_scale
    seg_ends = jnp.cumsum(span_lengths)
    places = jnp.arange(span_len, dtype=jnp.int32)
    segment = jnp.sum((places[:, None] >= seg_ends[None, :]).astype(jnp.int32), axis=1)
    allowed = (segment[:, None] == segment[None, :]) & (places[None, :] <= places[:, None])
    masked = jnp.where(allowed[None], scores, NEGATIVE)
    peak_score = jnp.max(masked, axis=2, keepdims=True)
    weights = jnp.exp(masked - peak_score)
    weight_sum = jnp.sum(weights, axis=2)
    mixed_out = jnp.einsum(
        "hqk,khd->qhd", weights.astype(jnp.bfloat16), values, preferred_element_type=jnp.float32
    )
    mixed_out = mixed_out / jnp.transpose(weight_sum)[:, :, None]
    return mixed_out.astype(jnp.bfloat16).reshape(span_len, head_count * head_size)


def plain_on_device(
    latent_rows,
    pre_queries,
    pre_lengths,
    owner_map,
    context_cache,
    context_lengths,
    new_latent,
    dec_queries,
    key_weight,
    value_weight,
):
    head_rank = lax.axis_index("head")
    batch_rank = lax.axis_index("batch")
    span_len = pre_queries.shape[0]
    kv_width = latent_rows.shape[1]
    own_span = lax.all_gather(latent_rows, "head", axis=0, tiled=True)
    other_span = from_partner(own_span, "batch", 0)
    first_span = jnp.where(batch_rank == 0, own_span, other_span)
    second_span = jnp.where(batch_rank == 0, other_span, own_span)
    all_spans = jnp.concatenate([first_span, second_span], axis=0)
    span_lengths = lax.dynamic_index_in_dim(pre_lengths, batch_rank, 0, keepdims=False)
    prefill_out = prefill_heads(own_span, pre_queries, span_lengths, key_weight, value_weight)
    step_total, rows_local, head_count, query_width = dec_queries.shape
    lat_width = key_weight.shape[0]
    head_size = key_weight.shape[1] // head_count
    owned_rows = context_cache.shape[0]
    score_scale = 1.0 / math.sqrt(query_width)
    key_heads = key_weight.reshape(lat_width, head_count, head_size)
    value_heads = value_weight.reshape(lat_width, head_count, head_size)
    absorbed = jnp.einsum(
        "srhd,lhd->srhl",
        dec_queries[..., :head_size],
        key_heads,
        preferred_element_type=jnp.float32,
    ).astype(jnp.bfloat16)
    query_all = jnp.concatenate([absorbed, dec_queries[..., head_size:]], axis=3)
    flat_owner, flat_start, flat_length = request_table(pre_lengths, owner_map, span_len)
    row_ids = (
        batch_rank * rows_local + head_rank * owned_rows + jnp.arange(owned_rows, dtype=jnp.int32)
    )
    matches = (flat_owner[None, :] == row_ids[:, None]).astype(jnp.int32)
    is_target = jnp.sum(matches, axis=1) > 0
    first_row = jnp.sum(matches * flat_start[None, :], axis=1)
    prompt_len = jnp.sum(matches * flat_length[None, :], axis=1)
    effective = jnp.where(is_target, prompt_len, context_lengths)
    padded = jnp.concatenate([all_spans, jnp.zeros((span_len, kv_width), all_spans.dtype)], axis=0)
    replaced = jax.vmap(lambda offset: lax.dynamic_slice_in_dim(padded, offset, span_len, 0))(
        first_row
    )
    front_rows = jnp.where(is_target[:, None, None], replaced, context_cache[:, :span_len])
    front_blocks = span_len // BLK
    needed = (jnp.max(effective) + BLK - 1) // BLK
    fresh_latent = new_latent[..., :lat_width]
    owned_query = lax.all_to_all(query_all, "head", split_axis=1, concat_axis=2, tiled=True)
    fresh_scores = (
        jnp.einsum("srhk,jrk->srhj", owned_query, new_latent, preferred_element_type=jnp.float32)
        * score_scale
    )
    visible = (
        jnp.arange(new_latent.shape[0], dtype=jnp.int32)[None, :]
        <= jnp.arange(step_total, dtype=jnp.int32)[:, None]
    )
    fresh_scores = jnp.where(visible[:, None, None, :], fresh_scores, NEGATIVE)
    peak_score = jnp.max(fresh_scores, axis=3)
    weights = jnp.exp(fresh_scores - peak_score[..., None])
    weight_sum = jnp.sum(weights, axis=3)
    running = jnp.einsum(
        "srhj,jrl->srhl",
        weights.astype(jnp.bfloat16),
        fresh_latent,
        preferred_element_type=jnp.float32,
    )

    def advance(block_index, state_tuple, source):
        old_peak, old_sum, old_running = state_tuple
        key_block = lax.dynamic_slice_in_dim(source, block_index * BLK, BLK, 1)
        scores = (
            jnp.einsum("srhk,rtk->srht", owned_query, key_block, preferred_element_type=jnp.float32)
            * score_scale
        )
        places = block_index * BLK + jnp.arange(BLK, dtype=jnp.int32)
        in_context = places[None, :] < effective[:, None]
        scores = jnp.where(in_context[None, :, None, :], scores, NEGATIVE)
        new_peak = jnp.maximum(old_peak, jnp.max(scores, axis=3))
        factor = jnp.exp(old_peak - new_peak)
        block_weights = jnp.exp(scores - new_peak[..., None])
        new_sum = old_sum * factor + jnp.sum(block_weights, axis=3)
        new_running = old_running * factor[..., None] + jnp.einsum(
            "srht,rtl->srhl",
            block_weights.astype(jnp.bfloat16),
            key_block[..., :lat_width],
            preferred_element_type=jnp.float32,
        )
        return (new_peak, new_sum, new_running)

    state_tuple = lax.fori_loop(
        0,
        jnp.minimum(needed, front_blocks),
        lambda block_index, state_now: advance(block_index, state_now, front_rows),
        (peak_score, weight_sum, running),
    )
    state_tuple = lax.fori_loop(
        front_blocks,
        jnp.maximum(needed, front_blocks),
        lambda block_index, state_now: advance(block_index, state_now, context_cache),
        state_tuple,
    )
    latent_out = (state_tuple[2] / state_tuple[1][..., None]).astype(jnp.bfloat16)
    returned = lax.all_to_all(latent_out, "head", split_axis=2, concat_axis=1, tiled=True)
    projected = jnp.einsum(
        "srhl,lhd->srhd", returned, value_heads, preferred_element_type=jnp.float32
    ).astype(jnp.bfloat16)
    decode_out = projected.reshape(query_all.shape[0], rows_local, head_count * head_size)
    return (prefill_out, decode_out)


def trans_dot(left, right):
    return lax.dot_general(
        left, right, (((1,), (1,)), ((), ())), preferred_element_type=jnp.float32
    )


MESH = pl.DeviceIdType.MESH


def place_of(rank, ranks):
    odd = rank % 2
    return (1 - odd) * (rank // 2) + odd * (ranks - 1 - rank // 2)


def rank_at(place, ranks):
    late = place // (ranks // 2)
    return (1 - late) * (2 * place) + late * (2 * (ranks - 1 - place) + 1)


def start_marks(ends, tail, vals, hot, tri):
    span_len, full = tail.shape
    marks = hot.shape[0]
    segs = len(ends)
    where = lax.broadcasted_iota(jnp.int32, (span_len, marks), 0)
    lane = lax.broadcasted_iota(jnp.int32, (span_len, marks), 1)
    place = lax.broadcasted_iota(jnp.int32, (marks, span_len), 1)
    line = lax.broadcasted_iota(jnp.int32, (marks, span_len), 0)
    mine = jnp.zeros((span_len, marks), jnp.int32)
    seen = jnp.zeros((marks, span_len), jnp.int32)
    for k in range(segs - 1):
        mine = mine + (where >= ends[k]).astype(jnp.int32)
        seen = seen + (place >= ends[k]).astype(jnp.int32)
    mark = jnp.where((lane < segs) & (lane != mine), NEGATIVE, 0.0).astype(jnp.bfloat16)
    hot[...] = jnp.where(line == seen, 1.0, 0.0).astype(jnp.bfloat16)
    tail[:, full - marks :] = mark
    for h in range(vals.shape[0]):
        vals[h, 128:, :] = jnp.ones((vals.shape[1] - 128, span_len), jnp.bfloat16)
    size = tri.shape[0]
    key_at = lax.broadcasted_iota(jnp.int32, (size, size), 0)
    query_at = lax.broadcasted_iota(jnp.int32, (size, size), 1)
    tri[...] = jnp.where(key_at <= query_at, 0.0, NEGATIVE)


def project_shard(origin, spans_ref, kw, vw, keys, vals, tail, lat, heads):
    own = spans_ref.shape[2]
    rows = jnp.transpose(spans_ref[origin])
    at = pl.ds(pl.multiple_of(origin * own, own), own)
    tail[at, : rows.shape[1] - lat] = rows[:, lat:]
    latent = rows[:, :lat]
    pair = 2
    for g in range(heads // pair):
        columns = slice(g * pair * 128, (g + 1) * pair * 128)
        key = jnp.dot(latent, kw[:, columns], preferred_element_type=jnp.float32)
        value = jnp.dot(latent, vw[:, columns], preferred_element_type=jnp.float32)
        key = key.astype(jnp.bfloat16)
        value = jnp.transpose(value.astype(jnp.bfloat16))
        for p in range(pair):
            h = g * pair + p
            keys[h, at, :] = key[:, p * 128 : (p + 1) * 128]
            vals[h, :128, at] = value[p * 128 : (p + 1) * 128]


def attention(g, pair, qs, keys, tail, vals, hot, tri, part_ref, scores, weights, look, scale):
    span_len = tail.shape[0]
    qb = tri.shape[0]
    blocks = span_len // qb
    order = [(0, p) for p in range(pair // 2)]
    order += [(i, p) for i in range(1, blocks) for p in range(pair)]
    order += [(0, p) for p in range(pair // 2, pair)]
    count = len(order)
    lengths = [min(i, look) + 1 for i, _ in order]
    peaks = [None] * count
    tops = [None] * count
    sums = [None] * count

    def score(n, c):
        i, p = order[n]
        if c > 0:
            return
        at = (i - lengths[n] + 1) * qb
        size = lengths[n] * qb
        query = jnp.concatenate(
            [qs[g * pair + p, :, i * qb : (i + 1) * qb], hot[:, i * qb : (i + 1) * qb]], axis=0
        )
        key = jnp.concatenate(
            [keys[g * pair + p, at : at + size, :], tail[at : at + size, :]], axis=1
        )
        s = jnp.dot(key, query, preferred_element_type=jnp.float32)
        if size > qb:
            scores[n % 4][: size - qb, :] = s[: size - qb]
            peaks[n] = jnp.max(s[: size - qb].reshape((size - qb) // 8, 8, qb), axis=0)
        last = s[size - qb :] + tri[...]
        scores[n % 4][size - qb : size, :] = last
        top = jnp.max(last.reshape(qb // 8, 8, qb), axis=0)
        peaks[n] = top if peaks[n] is None else jnp.maximum(peaks[n], top)

    def soften(n, c):
        if c == 0:
            tops[n] = jnp.max(peaks[n], axis=0, keepdims=True)
        for k in range(0, qb, 32):
            at = slice(c * qb + k, c * qb + k + 32)
            w = jnp.exp2((scores[n % 4][at, :] - tops[n]) * scale)
            weights[n % 4][at, :] = w.astype(jnp.bfloat16)

    def mix(n, c):
        i, p = order[n]
        at = (i - lengths[n] + 1) * qb
        if c == 0:
            o = jnp.dot(
                vals[g * pair + p, :, at : at + lengths[n] * qb],
                weights[n % 4][: lengths[n] * qb, :],
                preferred_element_type=jnp.float32,
            )
            o = o[:128] * (1.0 / o[128:129])
            columns = pl.ds(pl.multiple_of((g * pair + p) * 128, 128), 128)
            part_ref[i * qb : (i + 1) * qb, columns] = jnp.transpose(o.astype(jnp.bfloat16))

    todo_score = [(n, c) for n in range(count) for c in range(lengths[n])]
    todo_soft = list(todo_score)
    todo_mix = list(todo_score)
    scored = [0] * count
    softened = [0] * count
    mixed = [0] * count
    while todo_mix:
        was = list(softened)
        if todo_score:
            n, c = todo_score[0]
            if n < 4 or softened[n - 4] == lengths[n - 4]:
                score(n, c)
                scored[n] += 1
                todo_score.pop(0)
        if todo_soft:
            n, c = todo_soft[0]
            free = n < 4 or mixed[n - 4] == lengths[n - 4]
            if scored[n] == lengths[n] and free and not (todo_score and todo_score[0][0] <= n + 2):
                soften(n, c)
                softened[n] += 1
                todo_soft.pop(0)
        n, c = todo_mix[0]
        if was[n] == lengths[n]:
            mix(n, c)
            mixed[n] += 1
            todo_mix.pop(0)


def attend_groups(low, high, pair, qs, keys, tail, vals, hot, tri, part_ref, buffers, look, scale):
    scores, weights = buffers

    def step(g, carry):
        attention(
            g, pair, qs, keys, tail, vals, hot, tri, part_ref, scores, weights, look, scale
        )
        return carry

    lax.fori_loop(low, high, step, 0)


def absorb_into(dq, kw, sent, flat, wide, heads, lat):
    rows = dq.shape[0]
    ranks, owned, block, _ = sent.shape
    steps = block // heads
    local = ranks * owned
    flat[...] = dq[:, :128].astype(jnp.float32)
    for h in range(heads):
        mine = flat[pl.ds(h, rows // heads, stride=heads), :].astype(jnp.bfloat16)
        res = trans_dot(mine, kw[:, h * 128 : (h + 1) * 128])
        for s in range(steps):
            for c in range(lat // 128):
                wide[c, pl.ds(s * heads + h, local, stride=block), :] = res[
                    s * local : (s + 1) * local, c * 128 : (c + 1) * 128
                ]
    for p in range(ranks):
        for r in range(owned):
            at = p * owned + r
            for c in range(lat // 128):
                sent[p, r, :, c * 128 : (c + 1) * 128] = wide[
                    c, at * block : (at + 1) * block
                ].astype(jnp.bfloat16)
            for s in range(steps):
                start = (s * local + at) * heads
                sent[p, r, s * heads : (s + 1) * heads, lat:] = dq[start : start + heads, 128:]


def span_ends(lens_ref, batch_rank):
    ends = []
    total = 0
    for k in range(lens_ref.shape[1]):
        total = total + lens_ref[batch_rank, k]
        ends.append(total)
    return ends


def request_facts(lens_ref, owner_ref, ctx_ref, r, row, batch_rank, span_len):
    target = jnp.int32(0)
    first = jnp.int32(0)
    length = jnp.int32(0)
    spans = lens_ref.shape[0]
    for c in range(spans):
        start = jnp.int32(((c + spans) % spans) * span_len)
        for k in range(lens_ref.shape[1]):
            hit = (owner_ref[c, k] == row).astype(jnp.int32)
            target = target + hit
            first = first + hit * start
            length = length + hit * lens_ref[c, k]
            start = start + lens_ref[c, k]
    first = ((first + batch_rank * span_len) % (2 * span_len)) * target
    return first, length, ctx_ref[r] * (1 - target)


def decode_request(r, facts, got, new_ref, spans_ref, cache, lo, tools, *, lat, heads, steps, scale, blk):
    peak_ref, sum_ref, acc_ref, asked, scores, tops, weights, fades = tools
    ranks, _, block, kv = got.shape
    rows = ranks * block
    first, length, held = facts
    own = spans_ref.shape[2]
    full = asked.shape[1]
    piece = 256
    blocks = cache.shape[2] // blk
    spread = (full - kv) // 16
    tail = lax.broadcasted_iota(jnp.int32, (rows, full - kv), 1)
    lanes = lax.broadcasted_iota(jnp.int32, (rows, 128), 1)
    columns = lax.broadcasted_iota(jnp.int32, (16, piece), 1)

    def hidden(keep):
        return [jnp.where(keep, 0.0, NEGATIVE).astype(jnp.bfloat16)] * spread

    def begin():
        asked[:, :kv] = got[:, r].reshape(rows, kv)
        asked[:, kv:] = jnp.where(tail == 0, 1.0, 0.0).astype(jnp.bfloat16)
        newest = new_ref[...].astype(jnp.float32)
        fresh = jnp.concatenate(
            [newest[s, r : r + 1] for s in range(steps)]
            + [jnp.zeros((128 - steps, kv), jnp.float32)],
            axis=0,
        ).astype(jnp.bfloat16)
        s = trans_dot(asked[:, :kv], fresh)
        row_step = (lax.broadcasted_iota(jnp.int32, s.shape, 0) // heads) % steps
        s = jnp.where(lanes <= row_step, s, NEGATIVE)
        most = -(-(cache_front(spans_ref) + own - 1) // piece)
        base = jnp.minimum(first // own, spans_ref.shape[0] - most * (piece // own))
        top = s
        for c in range(most):
            at = base + c * (piece // own)
            shards = jnp.concatenate([spans_ref[at + i] for i in range(piece // own)], axis=1)
            place = at * own + columns
            keys = jnp.concatenate(
                [shards] + hidden((place >= first) & (place < first + length)), axis=0
            )
            part = jnp.dot(asked[...], keys, preferred_element_type=jnp.float32)
            scores[c // 2][:, (c % 2) * piece : (c % 2 + 1) * piece] = part
            top = jnp.maximum(top, jnp.maximum(part[:, :128], part[:, 128:]))
        m = jnp.max(top, axis=1, keepdims=True)
        peak_ref[...] = jnp.broadcast_to(m, peak_ref.shape)
        w = jnp.exp2((s - m) * scale)
        total = w
        acc = jnp.dot(w.astype(jnp.bfloat16), fresh[:, :lat], preferred_element_type=jnp.float32)
        for c in range(most):
            at = base + c * (piece // own)
            shards = jnp.concatenate(
                [spans_ref[at + i, :lat] for i in range(piece // own)], axis=1
            )
            w = jnp.exp2((scores[c // 2][:, (c % 2) * piece : (c % 2 + 1) * piece] - m) * scale)
            total = total + (w[:, :128] + w[:, 128:])
            acc = acc + trans_dot(w.astype(jnp.bfloat16), shards)
        sum_ref[...] = total
        acc_ref[...] = acc
        weights[1][...] = jnp.zeros(weights[1].shape, jnp.bfloat16)
        fades[1][...] = jnp.ones(fades[1].shape, jnp.float32)

    def score(t, side, c):
        at = pl.multiple_of(t * blk + c * piece, piece)
        keys = jnp.concatenate(
            [cache[r, :, pl.ds(at, piece)]] + hidden(at + columns < held), axis=0
        )
        s = jnp.dot(asked[...], keys, preferred_element_type=jnp.float32)
        scores[side][:, c * piece : (c + 1) * piece] = s
        top = jnp.maximum(s[:, :128], s[:, 128:])
        if c > 0:
            top = jnp.maximum(top, tops[side][...])
        tops[side][...] = top

    def settle(side):
        old = peak_ref[...]
        new = jnp.maximum(old, jnp.max(tops[side][...], axis=1, keepdims=True))
        fade = jnp.exp2((old - new) * scale)
        fades[side][...] = fade
        peak_ref[...] = new
        sum_ref[...] = sum_ref[...] * fade

    def soften(side, c):
        at = slice(c * piece, (c + 1) * piece)
        new = peak_ref[...]
        s = scores[side][:, at]
        left = jnp.exp2((s[:, :128] - new) * scale)
        right = jnp.exp2((s[:, 128:] - new) * scale)
        sum_ref[...] = sum_ref[...] + (left + right)
        weights[side][:, at] = jnp.concatenate([left, right], axis=1).astype(jnp.bfloat16)

    def mix(t, side, c):
        at = pl.multiple_of(jnp.maximum(t, 0) * blk, blk)
        some = slice(c * piece, (c + 1) * piece)
        made = trans_dot(weights[side][...], cache[r, some, pl.ds(at, blk)])
        fade = fades[side][...]
        for k in range(piece // 128):
            here = slice(c * piece + k * 128, c * piece + (k + 1) * 128)
            acc_ref[:, here] = acc_ref[:, here] * fade + made[:, k * 128 : (k + 1) * 128]

    def turn(j, carry):
        for side in range(2):
            t = 2 * j + side
            settle(side)
            for c in range(blk // piece):
                score(jnp.minimum(t + 1, blocks - 1), 1 - side, c)
                soften(side, c)
                mix(t - 1, 1 - side, c)
        return carry

    begin()
    for c in range(blk // piece):
        score(jnp.int32(0), 0, c)
    lax.fori_loop(0, blocks // 2, turn, 0)
    for c in range(lat // piece):
        mix(jnp.int32(blocks - 1), 1, c)
    total = jnp.sum(sum_ref[...], axis=1, keepdims=True)
    done = (acc_ref[...] * (1.0 / total)).astype(lo.dtype)
    for p in range(ranks):
        lo[p, r] = done[p * block : (p + 1) * block]


def cache_front(spans_ref):
    return spans_ref.shape[0] * spans_ref.shape[2] // 4


def serve_kernel(
    lens_ref, owner_ref, ctx_ref, new_ref, shard_hbm, dq_hbm, kw_hbm, vw_hbm, q_hbm, cache_hbm,
    back, part_ref,
    spans_ref, got, tail, hot, tri, kw, vw, qs, dq, flat, wide, sent, keys, vals, buffers, cache,
    lo, tools,
    load_sems, cache_sems, ring_send, ring_recv, swap_sems,
    give_sems, take_sems, back_send, back_recv,
    *, lat, ranks, heads, look, scale, pair, before, blk
):
    me = lax.axis_index("head")
    batch_rank = lax.axis_index("batch")
    place = place_of(me, ranks)
    right = rank_at((place + 1) % ranks, ranks)
    left = rank_at((place + ranks - 1) % ranks, ranks)
    owned = cache.shape[0]
    span_len = tail.shape[0]
    steps = sent.shape[2] // heads
    loads = [
        pltpu.make_async_copy(shard_hbm, spans_ref.at[me], load_sems.at[0]),
        pltpu.make_async_copy(dq_hbm, dq, load_sems.at[1]),
        pltpu.make_async_copy(kw_hbm, kw, load_sems.at[2]),
        pltpu.make_async_copy(vw_hbm, vw, load_sems.at[3]),
        pltpu.make_async_copy(q_hbm, qs, load_sems.at[4]),
    ] + [
        pltpu.make_async_copy(cache_hbm.at[r], cache.at[r], cache_sems.at[r])
        for r in range(owned)
    ]
    barrier = pltpu.get_barrier_semaphore()
    for k in range(1, ranks):
        pl.semaphore_signal(
            barrier, inc=1, device_id={"head": (me + k) % ranks}, device_id_type=MESH
        )
    pl.semaphore_signal(
        barrier, inc=1, device_id={"batch": 1 - batch_rank}, device_id_type=MESH
    )
    for load in loads:
        load.start()
    start_marks(span_ends(lens_ref, batch_rank), tail, vals, hot, tri)
    pl.semaphore_wait(barrier, ranks)

    half = shard_hbm.shape[0] // 2
    most = ranks // 2

    def hop(way, part, t):
        back_by = t - 1 if way == 0 else ranks - t + 1
        origin = rank_at((place + ranks - back_by) % ranks, ranks)
        rows = pl.ds(part * half, half)
        return pltpu.make_async_remote_copy(
            src_ref=spans_ref.at[origin, rows],
            dst_ref=spans_ref.at[origin, rows],
            send_sem=ring_send.at[way, part, t - 1],
            recv_sem=ring_recv.at[way, part, t - 1],
            device_id={"head": right if way == 0 else left},
            device_id_type=MESH,
        )

    def hops(way, part):
        return most if way == part else most - 1

    streams = [(0, 0), (1, 1), (0, 1), (1, 0)]
    loads[0].wait()
    for way, part in streams:
        hop(way, part, 1).start()
    loads[1].wait()
    loads[2].wait()
    absorb_into(dq, kw, sent, flat, wide, heads, lat)
    loads[3].wait()

    def project(origin):
        project_shard(origin, spans_ref, kw, vw, keys, vals, tail, lat, heads)

    def arrive(t, carry):
        for way, part in streams:
            if hops(way, part) == most:
                hop(way, part, t).wait_recv()
                pl.when(t < most)(lambda: hop(way, part, t + 1).start())
            else:

                @pl.when(t < most)
                def _():
                    hop(way, part, t).wait_recv()
                    pl.when(t < most - 1)(lambda: hop(way, part, t + 1).start())

        def one(side, carry):
            project(rank_at((place + side * t + (1 - side) * (ranks - t)) % ranks, ranks))
            return carry

        lax.fori_loop(0, 2 - t // most, one, 0)
        return carry

    project(me)
    lax.fori_loop(1, most + 1, arrive, 0)

    def exchange(source, target, r, send_sems, recv_sems):
        return [
            pltpu.make_async_remote_copy(
                src_ref=source.at[(me + k) % ranks, r],
                dst_ref=target.at[me, r],
                send_sem=send_sems.at[r, k - 1],
                recv_sem=recv_sems.at[r, k - 1],
                device_id={"head": (me + k) % ranks},
                device_id_type=MESH,
            )
            for k in range(1, ranks)
        ]

    gives = [exchange(sent, got, r, give_sems, take_sems) for r in range(owned)]
    backs = [exchange(lo, back, r, back_send, back_recv) for r in range(owned)]
    swap = pltpu.make_async_remote_copy(
        src_ref=spans_ref.at[:ranks],
        dst_ref=spans_ref.at[ranks:],
        send_sem=swap_sems.at[0],
        recv_sem=swap_sems.at[1],
        device_id={"batch": 1 - batch_rank},
        device_id_type=MESH,
    )
    for copies in gives:
        for copy in copies:
            copy.start()
    swap.start()
    keep = pltpu.make_async_copy(sent.at[me], got.at[me], load_sems.at[5])
    keep.start()
    loads[4].wait()

    def attend(low, high):
        attend_groups(
            low, high, pair, qs, keys, tail, vals, hot, tri, part_ref, buffers, look, scale
        )

    groups = heads // pair
    attend(0, before)
    keep.wait()
    swap.wait()
    for r in range(owned):
        for copy in gives[r]:
            copy.wait()
        loads[5 + r].wait()
        row = batch_rank * (ranks * owned) + me * owned + r
        facts = request_facts(lens_ref, owner_ref, ctx_ref, r, row, batch_rank, span_len)
        decode_request(
            r, facts, got, new_ref, spans_ref, cache, lo, tools[r],
            lat=lat, heads=heads, steps=steps, scale=scale, blk=blk,
        )
        for copy in backs[r]:
            copy.start()
    stay = pltpu.make_async_copy(lo.at[me], back.at[me], load_sems.at[6])
    stay.start()
    attend(before, groups)
    for way, part in streams:
        for t in range(1, hops(way, part) + 1):
            hop(way, part, t).wait_send()
    for copies in backs:
        for copy in copies:
            copy.wait()
    stay.wait()


HBM_SPEC = pl.BlockSpec(memory_space=pltpu.HBM)
VMEM_SPEC = pl.BlockSpec(memory_space=pltpu.VMEM)
SMEM_SPEC = pl.BlockSpec(memory_space=pltpu.SMEM)


def serve_pallas(lens, owner, ctx, newest, shard, flat_queries, key_weight, value_weight, turned, cache, ranks, qb=256, pair=4, before=2, blk=512, ahead=4):
    heads, width, span_len = turned.shape
    kv, own = shard.shape
    lat = key_weight.shape[0]
    rows = flat_queries.shape[0]
    owned = cache.shape[0]
    block = rows // (ranks * owned)
    look = min(-(-(span_len // 2) // qb), span_len // qb - 1)
    marks = 128 - (kv - lat)
    deep = (look + 1) * qb
    asks = ranks * block
    bf16, f32 = jnp.bfloat16, jnp.float32
    vmem, dma = pltpu.VMEM, pltpu.SemaphoreType.DMA
    return pl.pallas_call(
        functools.partial(
            serve_kernel,
            lat=lat,
            ranks=ranks,
            heads=heads,
            look=look,
            scale=math.log2(math.e) / math.sqrt(width),
            pair=pair,
            before=before,
            blk=blk,
        ),
        out_shape=(
            jax.ShapeDtypeStruct((ranks, owned, block, lat), bf16),
            jax.ShapeDtypeStruct((span_len, heads * 128), bf16),
        ),
        in_specs=[SMEM_SPEC] * 3 + [VMEM_SPEC] + [HBM_SPEC] * 6,
        out_specs=(VMEM_SPEC,) * 2,
        scratch_shapes=[
            vmem((2 * ranks, kv, own), bf16),
            vmem((ranks, owned, block, kv), bf16),
            vmem((span_len, 128), bf16),
            vmem((marks, span_len), bf16),
            vmem((qb, qb), f32),
            vmem(key_weight.shape, bf16),
            vmem(value_weight.shape, bf16),
            vmem((heads, width, span_len), bf16),
            vmem((rows, width), bf16),
            vmem((rows, 128), f32),
            vmem((lat // 128, rows, 128), f32),
            vmem((ranks, owned, block, kv), bf16),
            vmem((heads, span_len, 128), bf16),
            vmem((heads, 144, span_len), bf16),
            [[vmem((deep, qb), f32)] * ahead, [vmem((deep, qb), bf16)] * ahead],
            vmem(cache.shape, bf16),
            vmem((ranks, owned, block, lat), bf16),
            [
                [
                    vmem((asks, 128), f32),
                    vmem((asks, 128), f32),
                    vmem((asks, lat), f32),
                    vmem((asks, -(-(kv + 16) // 128) * 128), bf16),
                    [vmem((asks, blk), f32)] * 2,
                    [vmem((asks, 128), f32)] * 2,
                    [vmem((asks, blk), bf16)] * 2,
                    [vmem((asks, 128), f32)] * 2,
                ]
            ]
            * owned,
            dma((7,)),
            dma((owned,)),
            dma((2, 2, ranks // 2)),
            dma((2, 2, ranks // 2)),
            dma((2,)),
            dma((owned, ranks - 1)),
            dma((owned, ranks - 1)),
            dma((owned, ranks - 1)),
            dma((owned, ranks - 1)),
        ],
        compiler_params=pltpu.CompilerParams(
            collective_id=0, has_side_effects=True, vmem_limit_bytes=54 << 20
        ),
        cost_estimate=pl.CostEstimate(
            flops=30 * 10**9, bytes_accessed=24 << 20, transcendentals=14 << 20
        ),
    )(lens, owner, ctx, newest, shard, flat_queries, key_weight, value_weight, turned, cache)


def project_kernel(back_ref, vw_ref, part_ref, out_ref, whole_ref, wide, sems, *, heads, lat):
    ranks, owned, block, _ = back_ref.shape
    steps = block // heads
    local = ranks * owned
    shown = pltpu.make_async_copy(part_ref, whole_ref, sems.at[0])
    shown.start()
    for p in range(ranks):
        for r in range(owned):
            at = (p * owned + r) * block
            for c in range(lat // 128):
                wide[c, at : at + block] = back_ref[p, r, :, c * 128 : (c + 1) * 128].astype(
                    jnp.float32
                )
    for h in range(heads):
        mine = jnp.concatenate(
            [
                jnp.concatenate(
                    [
                        wide[c, pl.ds(s * heads + h, local, stride=block), :]
                        for c in range(lat // 128)
                    ],
                    axis=1,
                )
                for s in range(steps)
            ],
            axis=0,
        ).astype(jnp.bfloat16)
        out_ref[:, h * 128 : (h + 1) * 128] = jnp.dot(
            mine, vw_ref[:, h * 128 : (h + 1) * 128], preferred_element_type=jnp.float32
        ).astype(jnp.bfloat16)
    shown.wait()


def project_pallas(back, value_weight, part, heads):
    ranks, owned, block, lat = back.shape
    rows = ranks * owned * block
    return pl.pallas_call(
        functools.partial(project_kernel, heads=heads, lat=lat),
        out_shape=(
            jax.ShapeDtypeStruct((rows // heads, heads * 128), jnp.bfloat16),
            jax.ShapeDtypeStruct(part.shape, part.dtype),
        ),
        in_specs=[VMEM_SPEC, VMEM_SPEC, VMEM_SPEC],
        out_specs=(VMEM_SPEC, HBM_SPEC),
        scratch_shapes=[
            pltpu.VMEM((lat // 128, rows, 128), jnp.float32),
            pltpu.SemaphoreType.DMA((1,)),
        ],
        compiler_params=pltpu.CompilerParams(vmem_limit_bytes=8 << 20),
    )(back, value_weight, part)


def on_device(
    latent_rows,
    pre_queries,
    pre_lengths,
    owner_map,
    context_cache,
    context_lengths,
    new_latent,
    dec_queries,
    key_weight,
    value_weight,
):
    steps, rows_local, heads, width = dec_queries.shape
    ranks = lax.axis_size("head")
    if heads % 16 or latent_rows.shape[0] % 128 or ranks % 2:
        return plain_on_device(
            latent_rows,
            pre_queries,
            pre_lengths,
            owner_map,
            context_cache,
            context_lengths,
            new_latent,
            dec_queries,
            key_weight,
            value_weight,
        )
    stay = lambda x: pltpu.with_memory_space_constraint(x, pltpu.HBM)
    back, part = serve_pallas(
        pre_lengths,
        owner_map,
        context_lengths,
        new_latent,
        stay(jnp.transpose(latent_rows)),
        stay(dec_queries.reshape(-1, width)),
        stay(key_weight),
        stay(value_weight),
        stay(jnp.transpose(pre_queries, (1, 2, 0))),
        stay(jnp.transpose(context_cache, (0, 2, 1))),
        ranks,
    )
    decode_out, prefill_out = project_pallas(back, value_weight, part, heads)
    return (prefill_out, decode_out.reshape(steps, rows_local, heads * 128))


def solution(mesh):
    placed = (
        P(("groups", "batch", "head"), None),
        P(("groups", "batch"), "head", None),
        P("groups", None),
        P("groups", None),
        P(("groups", "batch", "head"), None, None),
        P(("groups", "batch", "head")),
        P("groups", ("batch", "head"), None),
        P("groups", "batch", "head", None),
        P(None, "head"),
        P(None, "head"),
    )
    return jax.shard_map(
        on_device,
        mesh=mesh,
        in_specs=placed,
        out_specs=(P(("groups", "batch"), "head"), P("groups", "batch", "head")),
        check_vma=False,
    )
```

profile of v0, /device:TPU:0, one launch (start us, length us, event | category | flops | bytes accessed | tf_op | source)
XLA Modules:
  0.0 60.8 jit_solution(12358304186329846598)
XLA Ops:
  0.6 0.0 copy-start.1
  0.6 53.0 %shard_map.113 = (bf16[8,2,32,512]{3,2,1,0:T(8,128)(2,1)}, bf16[1024,2048]{1,0:T(8,128)(2,1)}) custom-call(s32[2,4]{1,0:T(2,128)} %lens_ref.1, s32[2,4]{1,0:T(2,128)} %owner_ref.1, s32[2]{0:T(128)} %ctx_ref.1, bf16[2,2,576]{2,1,0:T(2,128)(2,1)} %new_ref.1, bf16[576,128]{1,0:T(8,128)(2,1)} %bitcast.8, bf16[512,192]{1,0:T(8,128)(2,1)} %bitcast.7, ...), custom_call_target="tpu_custom_call" | custom-call | flops 30000001024 | bytes 25165824 | tf_op jit(solution)/shard_map/pallas_call | solution.py:694
  53.6 0.0 copy-done.1
  53.6 0.0 copy-start
  53.6 2.2 %copy-done = bf16[1024,2048]{1,0:T(8,128)(2,1)S(1)} copy-done((bf16[1024,2048]{1,0:T(8,128)(2,1)S(1)}, bf16[1024,2048]{1,0:T(8,128)(2,1)}, u32[]{:S(2)}) %copy-start) | copy-done | bytes 4194328
  55.8 0.0 copy-start.2
  55.8 1.0 %copy-done.2 = bf16[8,2,32,512]{3,2,1,0:T(8,128)(2,1)S(1)} copy-done((bf16[8,2,32,512]{3,2,1,0:T(8,128)(2,1)S(1)}, bf16[8,2,32,512]{3,2,1,0:T(8,128)(2,1)}, u32[]{:S(2)}) %copy-start.2) | copy-done | bytes 524312
  56.9 3.8 %shard_map.114 = (bf16[32,2048]{1,0:T(8,128)(2,1)}, bf16[1024,2048]{1,0:T(8,128)(2,1)}) custom-call(bf16[8,2,32,512]{3,2,1,0:T(8,128)(2,1)S(1)} %copy-done.2, bf16[512,2048]{1,0:T(8,128)(2,1)S(1)} %copy-done.1, bf16[1024,2048]{1,0:T(8,128)(2,1)S(1)} %copy-done), custom_call_target="tpu_custom_call" | custom-call | tf_op jit(solution)/shard_map/pallas_call | solution.py:798
Async XLA Ops:
  0.6 53.0 %copy-start.1 = (bf16[512,2048]{1,0:T(8,128)(2,1)S(1)}, bf16[512,2048]{1,0:T(8,128)(2,1)}, u32[]{:S(2)}) copy-start(bf16[512,2048]{1,0:T(8,128)(2,1)} %vw_ref.1) | copy-start | bytes 6291460
  53.6 2.2 %copy-start = (bf16[1024,2048]{1,0:T(8,128)(2,1)S(1)}, bf16[1024,2048]{1,0:T(8,128)(2,1)}, u32[]{:S(2)}) copy-start(bf16[1024,2048]{1,0:T(8,128)(2,1)} %get-tuple-element.7.part_ref) | copy-start | bytes 12582916
  55.8 1.0 %copy-start.2 = (bf16[8,2,32,512]{3,2,1,0:T(8,128)(2,1)S(1)}, bf16[8,2,32,512]{3,2,1,0:T(8,128)(2,1)}, u32[]{:S(2)}) copy-start(bf16[8,2,32,512]{3,2,1,0:T(8,128)(2,1)} %get-tuple-element.6.back_ref) | copy-start | bytes 1572868
where the time goes:
time: 61 us; the launch traced here: 60.8 us
  Pallas kernels  56.7 us (93%)
  local copies, waits for them, and re-layouts  3.23 us (5%)
  between operations  0.83 us (1%)
    pallas_call x1, Pallas kernels, serve_pallas(): pl.pallas_call(functools.partial(serve_kernel, lat=lat, ranks=ranks, head...  53 us
    pallas_call x1, Pallas kernels, project_pallas(): pl.pallas_call(functools.partial(project_kernel, heads=heads, lat=lat), o...  3.76 us
    unnamed x6, local copies, waits for them, and re-layouts  3.23 us

commit v1 on v0

--- a/solution.py
+++ b/solution.py
@@ -517,11 +517,11 @@
 
 
 def serve_kernel(
-    lens_ref, owner_ref, ctx_ref, new_ref, shard_hbm, dq_hbm, kw_hbm, vw_hbm, q_hbm, cache_hbm,
+    lens_hbm, owner_hbm, ctx_hbm, new_hbm, shard_hbm, dq_hbm, kw_hbm, vw_hbm, q_hbm, cache_hbm,
     back, part_ref,
     spans_ref, got, tail, hot, tri, kw, vw, qs, dq, flat, wide, sent, keys, vals, buffers, cache,
-    lo, tools,
-    load_sems, cache_sems, ring_send, ring_recv, swap_sems,
+    lo, tools, lens_ref, owner_ref, ctx_ref, new_ref,
+    load_sems, cache_sems, small_sems, ring_send, ring_recv, swap_sems,
     give_sems, take_sems, back_send, back_recv,
     *, lat, ranks, heads, look, scale, pair, before, blk
 ):
@@ -551,8 +551,16 @@
     pl.semaphore_signal(
         barrier, inc=1, device_id={"batch": 1 - batch_rank}, device_id_type=MESH
     )
-    for load in loads:
+    smalls = [
+        pltpu.make_async_copy(lens_hbm, lens_ref, small_sems.at[0]),
+        pltpu.make_async_copy(owner_hbm, owner_ref, small_sems.at[1]),
+        pltpu.make_async_copy(ctx_hbm, ctx_ref, small_sems.at[2]),
+        pltpu.make_async_copy(new_hbm, new_ref, small_sems.at[3]),
+    ]
+    for load in smalls + loads:
         load.start()
+    for small in smalls:
+        small.wait()
     start_marks(span_ends(lens_ref, batch_rank), tail, vals, hot, tri)
     pl.semaphore_wait(barrier, ranks)
 
@@ -656,7 +664,7 @@
         row = batch_rank * (ranks * owned) + me * owned + r
         facts = request_facts(lens_ref, owner_ref, ctx_ref, r, row, batch_rank, span_len)
         decode_request(
-            r, facts, got, new_ref, spans_ref, cache, lo, tools[r],
+            r, facts, got, new_ref, spans_ref, cache, lo, tools,
             lat=lat, heads=heads, steps=steps, scale=scale, blk=blk,
         )
         for copy in backs[r]:
@@ -707,7 +715,7 @@
             jax.ShapeDtypeStruct((ranks, owned, block, lat), bf16),
             jax.ShapeDtypeStruct((span_len, heads * 128), bf16),
         ),
-        in_specs=[SMEM_SPEC] * 3 + [VMEM_SPEC] + [HBM_SPEC] * 6,
+        in_specs=[HBM_SPEC] * 10,
         out_specs=(VMEM_SPEC,) * 2,
         scratch_shapes=[
             vmem((2 * ranks, kv, own), bf16),
@@ -728,20 +736,22 @@
             vmem(cache.shape, bf16),
             vmem((ranks, owned, block, lat), bf16),
             [
-                [
-                    vmem((asks, 128), f32),
-                    vmem((asks, 128), f32),
-                    vmem((asks, lat), f32),
-                    vmem((asks, -(-(kv + 16) // 128) * 128), bf16),
-                    [vmem((asks, blk), f32)] * 2,
-                    [vmem((asks, 128), f32)] * 2,
-                    [vmem((asks, blk), bf16)] * 2,
-                    [vmem((asks, 128), f32)] * 2,
-                ]
-            ]
-            * owned,
+                vmem((asks, 128), f32),
+                vmem((asks, 128), f32),
+                vmem((asks, lat), f32),
+                vmem((asks, -(-(kv + 16) // 128) * 128), bf16),
+                [vmem((asks, blk), f32)] * 2,
+                [vmem((asks, 128), f32)] * 2,
+                [vmem((asks, blk), bf16)] * 2,
+                [vmem((asks, 128), f32)] * 2,
+            ],
+            pltpu.SMEM(lens.shape, lens.dtype),
+            pltpu.SMEM(owner.shape, owner.dtype),
+            pltpu.SMEM(ctx.shape, ctx.dtype),
+            vmem(newest.shape, newest.dtype),
             dma((7,)),
             dma((owned,)),
+            dma((4,)),
             dma((2, 2, ranks // 2)),
             dma((2, 2, ranks // 2)),
             dma((2,)),
@@ -751,7 +761,7 @@
             dma((owned, ranks - 1)),
         ],
         compiler_params=pltpu.CompilerParams(
-            collective_id=0, has_side_effects=True, vmem_limit_bytes=54 << 20
+            collective_id=0, has_side_effects=True, vmem_limit_bytes=46 << 20
         ),
         cost_estimate=pl.CostEstimate(
             flops=30 * 10**9, bytes_accessed=24 << 20, transcendentals=14 << 20
@@ -840,10 +850,10 @@
         )
     stay = lambda x: pltpu.with_memory_space_constraint(x, pltpu.HBM)
     back, part = serve_pallas(
-        pre_lengths,
-        owner_map,
-        context_lengths,
-        new_latent,
+        stay(pre_lengths),
+        stay(owner_map),
+        stay(context_lengths),
+        stay(new_latent),
         stay(jnp.transpose(latent_rows)),
         stay(dec_queries.reshape(-1, width)),
         stay(key_weight),

time: 61 us -> 56.7 us (0.930)
  local copies, waits for them, and re-layouts: 3.23 us -> 0.01 us
  Pallas kernels: 56.7 us -> 55.6 us
    unnamed x6 -> x2, local copies, waits for them, and re-layouts: 3.23 us -> 0.01 us
    pallas_call x1, Pallas kernels: 53 us -> 51.8 us  [serve_pallas(): pl.pallas_call(functools.partial(serve_kernel, lat=lat, ranks=ranks, head...]
where the time goes in v1:
time: 56.7 us; the launch traced here: 56.4 us
  Pallas kernels  55.6 us (98%)
  between operations  0.82 us (1%)
    pallas_call x1, Pallas kernels, serve_pallas(): pl.pallas_call(functools.partial(serve_kernel, lat=lat, ranks=ranks, head...  51.8 us
    pallas_call x1, Pallas kernels, project_pallas(): pl.pallas_call(functools.partial(project_kernel, heads=heads, lat=lat), o...  3.76 us

profile of v1, /device:TPU:0, one launch (start us, length us, event | category | flops | bytes accessed | tf_op | source)
XLA Modules:
  0.0 56.4 jit_solution(10827984022074381296)
XLA Ops:
  0.6 0.0 copy-start
  0.6 51.8 %shard_map.113 = (bf16[8,2,32,512]{3,2,1,0:T(8,128)(2,1)S(1)}, bf16[1024,2048]{1,0:T(8,128)(2,1)S(1)}) custom-call(s32[2,4]{1,0:T(2,128)} %lens_hbm.1, s32[2,4]{1,0:T(2,128)} %owner_hbm.1, s32[2]{0:T(128)} %ctx_hbm.1, bf16[2,2,576]{2,1,0:T(2,128)(2,1)} %new_hbm.1, bf16[576,128]{1,0:T(8,128)(2,1)} %bitcast.8, bf16[512,192]{1,0:T(8,128)(2,1)} %bitcast.7, ...), custom_call_target="tpu_custom_call" | custom-call | flops 30000001024 | bytes 25165824 | tf_op jit(solution)/shard_map/pallas_call | solution.py:702
  52.5 0.0 copy-done
  52.5 3.8 %shard_map.114 = (bf16[32,2048]{1,0:T(8,128)(2,1)}, bf16[1024,2048]{1,0:T(8,128)(2,1)}) custom-call(bf16[8,2,32,512]{3,2,1,0:T(8,128)(2,1)S(1)} %get-tuple-element.6.back_ref, bf16[512,2048]{1,0:T(8,128)(2,1)S(1)} %copy-done, bf16[1024,2048]{1,0:T(8,128)(2,1)S(1)} %get-tuple-element.7.part_ref), custom_call_target="tpu_custom_call" | custom-call | tf_op jit(solution)/shard_map/pallas_call | solution.py:808
Async XLA Ops:
  0.6 51.9 %copy-start = (bf16[512,2048]{1,0:T(8,128)(2,1)S(1)}, bf16[512,2048]{1,0:T(8,128)(2,1)}, u32[]{:S(2)}) copy-start(bf16[512,2048]{1,0:T(8,128)(2,1)} %vw_ref.1) | copy-start | bytes 6291460

commit v2 on v1

--- a/solution.py
+++ b/solution.py
@@ -403,50 +403,63 @@
     blocks = cache.shape[2] // blk
     spread = (full - kv) // 16
     tail = lax.broadcasted_iota(jnp.int32, (rows, full - kv), 1)
-    lanes = lax.broadcasted_iota(jnp.int32, (rows, 128), 1)
     columns = lax.broadcasted_iota(jnp.int32, (16, piece), 1)
 
+    line = lax.broadcasted_iota(jnp.int32, (16, piece), 0)
+
     def hidden(keep):
-        return [jnp.where(keep, 0.0, NEGATIVE).astype(jnp.bfloat16)] * spread
+        mask = jnp.where((line == 0) & jnp.logical_not(keep), NEGATIVE, 0.0)
+        return [mask.astype(jnp.bfloat16)] * spread
 
     def begin():
         asked[:, :kv] = got[:, r].reshape(rows, kv)
-        asked[:, kv:] = jnp.where(tail == 0, 1.0, 0.0).astype(jnp.bfloat16)
+        row_step = (lax.broadcasted_iota(jnp.int32, tail.shape, 0) // heads) % steps
+        asked[:, kv:] = jnp.where((tail == 0) | (tail == row_step + 1), 1.0, 0.0).astype(
+            jnp.bfloat16
+        )
         newest = new_ref[...].astype(jnp.float32)
         fresh = jnp.concatenate(
             [newest[s, r : r + 1] for s in range(steps)]
-            + [jnp.zeros((128 - steps, kv), jnp.float32)],
+            + [jnp.zeros((own - steps, kv), jnp.float32)],
             axis=0,
         ).astype(jnp.bfloat16)
-        s = trans_dot(asked[:, :kv], fresh)
-        row_step = (lax.broadcasted_iota(jnp.int32, s.shape, 0) // heads) % steps
-        s = jnp.where(lanes <= row_step, s, NEGATIVE)
-        most = -(-(cache_front(spans_ref) + own - 1) // piece)
-        base = jnp.minimum(first // own, spans_ref.shape[0] - most * (piece // own))
-        top = s
+        fresh = jnp.transpose(fresh)
+        span_len = spans_ref.shape[0] * own // 2
+        shards = -(-(span_len // 2 + own - 1) // own)
+        base = jnp.minimum(first // own, spans_ref.shape[0] - shards)
+        each = piece // own
+        most = (shards + 1) // each
+
+        def block(c):
+            parts = []
+            for i in range(c * each, (c + 1) * each):
+                parts.append(spans_ref[base + i] if i < shards else fresh)
+            return jnp.concatenate(parts, axis=1)
+
+        top = None
         for c in range(most):
-            at = base + c * (piece // own)
-            shards = jnp.concatenate([spans_ref[at + i] for i in range(piece // own)], axis=1)
-            place = at * own + columns
-            keys = jnp.concatenate(
-                [shards] + hidden((place >= first) & (place < first + length)), axis=0
-            )
+            place = (base + c * each) * own + columns
+            keep = (place >= first) & (place < first + length)
+            mask = jnp.where((line == 0) & jnp.logical_not(keep), NEGATIVE, 0.0)
+            if c == most - 1:
+                new_at = columns - (piece - own)
+                late = (line == 0) & (new_at >= steps)
+                late = late | ((line > 0) & (new_at > line - 1))
+                mask = jnp.where(new_at >= 0, jnp.where(late, NEGATIVE, 0.0), mask)
+            keys = jnp.concatenate([block(c)] + [mask.astype(jnp.bfloat16)] * spread, axis=0)
             part = jnp.dot(asked[...], keys, preferred_element_type=jnp.float32)
             scores[c // 2][:, (c % 2) * piece : (c % 2 + 1) * piece] = part
-            top = jnp.maximum(top, jnp.maximum(part[:, :128], part[:, 128:]))
+            best = jnp.maximum(part[:, :128], part[:, 128:])
+            top = best if top is None else jnp.maximum(top, best)
         m = jnp.max(top, axis=1, keepdims=True)
         peak_ref[...] = jnp.broadcast_to(m, peak_ref.shape)
-        w = jnp.exp2((s - m) * scale)
-        total = w
-        acc = jnp.dot(w.astype(jnp.bfloat16), fresh[:, :lat], preferred_element_type=jnp.float32)
+        total, acc = None, None
         for c in range(most):
-            at = base + c * (piece // own)
-            shards = jnp.concatenate(
-                [spans_ref[at + i, :lat] for i in range(piece // own)], axis=1
-            )
             w = jnp.exp2((scores[c // 2][:, (c % 2) * piece : (c % 2 + 1) * piece] - m) * scale)
-            total = total + (w[:, :128] + w[:, 128:])
-            acc = acc + trans_dot(w.astype(jnp.bfloat16), shards)
+            both = w[:, :128] + w[:, 128:]
+            made = trans_dot(w.astype(jnp.bfloat16), block(c)[:lat])
+            total = both if total is None else total + both
+            acc = made if acc is None else acc + made
         sum_ref[...] = total
         acc_ref[...] = acc
         weights[1][...] = jnp.zeros(weights[1].shape, jnp.bfloat16)
@@ -495,25 +508,23 @@
             t = 2 * j + side
             settle(side)
             for c in range(blk // piece):
-                score(jnp.minimum(t + 1, blocks - 1), 1 - side, c)
+                if not (isinstance(t, int) and t + 1 == blocks):
+                    score(t + 1, 1 - side, c)
                 soften(side, c)
                 mix(t - 1, 1 - side, c)
         return carry
 
     begin()
     for c in range(blk // piece):
-        score(jnp.int32(0), 0, c)
-    lax.fori_loop(0, blocks // 2, turn, 0)
+        score(0, 0, c)
+    lax.fori_loop(0, blocks // 2 - 1, turn, 0)
+    turn(blocks // 2 - 1, 0)
     for c in range(lat // piece):
-        mix(jnp.int32(blocks - 1), 1, c)
+        mix(blocks - 1, 1, c)
     total = jnp.sum(sum_ref[...], axis=1, keepdims=True)
     done = (acc_ref[...] * (1.0 / total)).astype(lo.dtype)
     for p in range(ranks):
         lo[p, r] = done[p * block : (p + 1) * block]
-
-
-def cache_front(spans_ref):
-    return spans_ref.shape[0] * spans_ref.shape[2] // 4
 
 
 def serve_kernel(
@@ -564,13 +575,13 @@
     start_marks(span_ends(lens_ref, batch_rank), tail, vals, hot, tri)
     pl.semaphore_wait(barrier, ranks)
 
-    half = shard_hbm.shape[0] // 2
+    quarter = shard_hbm.shape[0] // 4
     most = ranks // 2
 
     def hop(way, part, t):
         back_by = t - 1 if way == 0 else ranks - t + 1
         origin = rank_at((place + ranks - back_by) % ranks, ranks)
-        rows = pl.ds(part * half, half)
+        rows = pl.ds(part * quarter, quarter)
         return pltpu.make_async_remote_copy(
             src_ref=spans_ref.at[origin, rows],
             dst_ref=spans_ref.at[origin, rows],
@@ -581,9 +592,9 @@
         )
 
     def hops(way, part):
-        return most if way == part else most - 1
-
-    streams = [(0, 0), (1, 1), (0, 1), (1, 0)]
+        return most if way == part // 2 else most - 1
+
+    streams = [(0, 0), (1, 2), (0, 1), (1, 3), (0, 2), (1, 0), (0, 3), (1, 1)]
     loads[0].wait()
     for way, part in streams:
         hop(way, part, 1).start()
@@ -752,8 +763,8 @@
             dma((7,)),
             dma((owned,)),
             dma((4,)),
-            dma((2, 2, ranks // 2)),
-            dma((2, 2, ranks // 2)),
+            dma((2, 4, ranks // 2)),
+            dma((2, 4, ranks // 2)),
             dma((2,)),
             dma((owned, ranks - 1)),
             dma((owned, ranks - 1)),
@@ -782,23 +793,30 @@
                 wide[c, at : at + block] = back_ref[p, r, :, c * 128 : (c + 1) * 128].astype(
                     jnp.float32
                 )
-    for h in range(heads):
-        mine = jnp.concatenate(
-            [
-                jnp.concatenate(
-                    [
-                        wide[c, pl.ds(s * heads + h, local, stride=block), :]
-                        for c in range(lat // 128)
-                    ],
-                    axis=1,
-                )
-                for s in range(steps)
-            ],
-            axis=0,
-        ).astype(jnp.bfloat16)
-        out_ref[:, h * 128 : (h + 1) * 128] = jnp.dot(
-            mine, vw_ref[:, h * 128 : (h + 1) * 128], preferred_element_type=jnp.float32
-        ).astype(jnp.bfloat16)
+
+    def some_heads(g, carry):
+        for p in range(4):
+            h = g * 4 + p
+            mine = jnp.concatenate(
+                [
+                    jnp.concatenate(
+                        [
+                            wide[c, pl.ds(s * heads + h, local, stride=block), :]
+                            for c in range(lat // 128)
+                        ],
+                        axis=1,
+                    )
+                    for s in range(steps)
+                ],
+                axis=0,
+            ).astype(jnp.bfloat16)
+            columns = pl.ds(pl.multiple_of(h * 128, 128), 128)
+            out_ref[:, columns] = jnp.dot(
+                mine, vw_ref[:, columns], preferred_element_type=jnp.float32
+            ).astype(jnp.bfloat16)
+        return carry
+
+    lax.fori_loop(0, heads // 4, some_heads, 0)
     shown.wait()
 
 

time: 56.7 us -> 54.4 us (0.959)
  Pallas kernels: 55.6 us -> 52.9 us
    pallas_call x1, Pallas kernels: 51.8 us -> 50.2 us  [serve_pallas(): pl.pallas_call(functools.partial(serve_kernel, lat=lat, ranks=ranks, head...]
    pallas_call x1, Pallas kernels: 3.76 us -> 2.68 us  [project_pallas(): pl.pallas_call(functools.partial(project_kernel, heads=heads, lat=lat), o...]
where the time goes in v2:
time: 54.4 us; the launch traced here: 53.7 us
  Pallas kernels  52.9 us (97%)
  between operations  0.84 us (2%)
    pallas_call x1, Pallas kernels, serve_pallas(): pl.pallas_call(functools.partial(serve_kernel, lat=lat, ranks=ranks, head...  50.2 us
    pallas_call x1, Pallas kernels, project_pallas(): pl.pallas_call(functools.partial(project_kernel, heads=heads, lat=lat), o...  2.68 us

profile of v2, /device:TPU:0, one launch (start us, length us, event | category | flops | bytes accessed | tf_op | source)
XLA Modules:
  0.0 53.7 jit_solution(11448686300807827544)
XLA Ops:
  0.6 0.0 copy-start
  0.6 50.2 %shard_map.113 = (bf16[8,2,32,512]{3,2,1,0:T(8,128)(2,1)S(1)}, bf16[1024,2048]{1,0:T(8,128)(2,1)S(1)}) custom-call(s32[2,4]{1,0:T(2,128)} %lens_hbm.1, s32[2,4]{1,0:T(2,128)} %owner_hbm.1, s32[2]{0:T(128)} %ctx_hbm.1, bf16[2,2,576]{2,1,0:T(2,128)(2,1)} %new_hbm.1, bf16[576,128]{1,0:T(8,128)(2,1)} %bitcast.8, bf16[512,192]{1,0:T(8,128)(2,1)} %bitcast.7, ...), custom_call_target="tpu_custom_call" | custom-call | flops 30000001024 | bytes 25165824 | tf_op jit(solution)/shard_map/pallas_call | solution.py:713
  50.9 0.0 copy-done
  50.9 2.7 %shard_map.114 = (bf16[32,2048]{1,0:T(8,128)(2,1)}, bf16[1024,2048]{1,0:T(8,128)(2,1)}) custom-call(bf16[8,2,32,512]{3,2,1,0:T(8,128)(2,1)S(1)} %get-tuple-element.6.back_ref, bf16[512,2048]{1,0:T(8,128)(2,1)S(1)} %copy-done, bf16[1024,2048]{1,0:T(8,128)(2,1)S(1)} %get-tuple-element.7.part_ref), custom_call_target="tpu_custom_call" | custom-call | tf_op jit(solution)/shard_map/pallas_call | solution.py:826
Async XLA Ops:
  0.6 50.2 %copy-start = (bf16[512,2048]{1,0:T(8,128)(2,1)S(1)}, bf16[512,2048]{1,0:T(8,128)(2,1)}, u32[]{:S(2)}) copy-start(bf16[512,2048]{1,0:T(8,128)(2,1)} %vw_ref.1) | copy-start | bytes 6291460

commit v3 on v2

--- a/solution.py
+++ b/solution.py
@@ -226,14 +226,17 @@
     tri[...] = jnp.where(key_at <= query_at, 0.0, NEGATIVE)
 
 
-def project_shard(origin, spans_ref, kw, vw, keys, vals, tail, lat, heads):
+def project_piece(slot, origin, piece, pieces, spans_ref, held, kw, vw, keys, vals, tail, lat, heads):
     own = spans_ref.shape[2]
-    rows = jnp.transpose(spans_ref[origin])
     at = pl.ds(pl.multiple_of(origin * own, own), own)
-    tail[at, : rows.shape[1] - lat] = rows[:, lat:]
-    latent = rows[:, :lat]
+    if piece == 0:
+        rows = jnp.transpose(spans_ref[origin])
+        held[slot] = rows
+        tail[at, : rows.shape[1] - lat] = rows[:, lat:]
+    latent = held[slot, :, :lat]
     pair = 2
-    for g in range(heads // pair):
+    each = heads // pair // pieces
+    for g in range(piece * each, (piece + 1) * each):
         columns = slice(g * pair * 128, (g + 1) * pair * 128)
         key = jnp.dot(latent, kw[:, columns], preferred_element_type=jnp.float32)
         value = jnp.dot(latent, vw[:, columns], preferred_element_type=jnp.float32)
@@ -340,20 +343,24 @@
     lax.fori_loop(low, high, step, 0)
 
 
-def absorb_into(dq, kw, sent, flat, wide, heads, lat):
-    rows = dq.shape[0]
+def absorb_heads(low, high, kw, sent, flat, wide, heads, lat):
     ranks, owned, block, _ = sent.shape
     steps = block // heads
     local = ranks * owned
-    flat[...] = dq[:, :128].astype(jnp.float32)
-    for h in range(heads):
-        mine = flat[pl.ds(h, rows // heads, stride=heads), :].astype(jnp.bfloat16)
+    for h in range(low, high):
+        mine = flat[pl.ds(h, steps * local, stride=heads), :].astype(jnp.bfloat16)
         res = trans_dot(mine, kw[:, h * 128 : (h + 1) * 128])
         for s in range(steps):
             for c in range(lat // 128):
                 wide[c, pl.ds(s * heads + h, local, stride=block), :] = res[
                     s * local : (s + 1) * local, c * 128 : (c + 1) * 128
                 ]
+
+
+def absorb_finish(dq, sent, wide, heads, lat):
+    ranks, owned, block, _ = sent.shape
+    steps = block // heads
+    local = ranks * owned
     for p in range(ranks):
         for r in range(owned):
             at = p * owned + r
@@ -531,7 +538,7 @@
     lens_hbm, owner_hbm, ctx_hbm, new_hbm, shard_hbm, dq_hbm, kw_hbm, vw_hbm, q_hbm, cache_hbm,
     back, part_ref,
     spans_ref, got, tail, hot, tri, kw, vw, qs, dq, flat, wide, sent, keys, vals, buffers, cache,
-    lo, tools, lens_ref, owner_ref, ctx_ref, new_ref,
+    lo, tools, held, lens_ref, owner_ref, ctx_ref, new_ref,
     load_sems, cache_sems, small_sems, ring_send, ring_recv, swap_sems,
     give_sems, take_sems, back_send, back_recv,
     *, lat, ranks, heads, look, scale, pair, before, blk
@@ -598,16 +605,31 @@
     loads[0].wait()
     for way, part in streams:
         hop(way, part, 1).start()
+    loads[2].wait()
+    loads[3].wait()
+    pieces = 4
+
+    def project(slot, origin, piece):
+        project_piece(
+            slot, origin, piece, pieces, spans_ref, held, kw, vw, keys, vals, tail, lat, heads
+        )
+
+    for piece in range(pieces):
+        project(0, me, piece)
     loads[1].wait()
-    loads[2].wait()
-    absorb_into(dq, kw, sent, flat, wide, heads, lat)
-    loads[3].wait()
-
-    def project(origin):
-        project_shard(origin, spans_ref, kw, vw, keys, vals, tail, lat, heads)
+    flat[...] = dq[:, :128].astype(jnp.float32)
+    each = heads // pieces
+    for i, (way, part) in enumerate(streams):
+        hop(way, part, 1).wait_recv()
+        hop(way, part, 2).start()
+        if i < pieces:
+            absorb_heads(i * each, (i + 1) * each, kw, sent, flat, wide, heads, lat)
+        if i == pieces:
+            absorb_finish(dq, sent, wide, heads, lat)
 
     def arrive(t, carry):
-        for way, part in streams:
+        near = [rank_at((place + ranks - t + 1) % ranks, ranks), rank_at((place + t - 1) % ranks, ranks)]
+        for i, (way, part) in enumerate(streams):
             if hops(way, part) == most:
                 hop(way, part, t).wait_recv()
                 pl.when(t < most)(lambda: hop(way, part, t + 1).start())
@@ -618,15 +640,12 @@
                     hop(way, part, t).wait_recv()
                     pl.when(t < most - 1)(lambda: hop(way, part, t + 1).start())
 
-        def one(side, carry):
-            project(rank_at((place + side * t + (1 - side) * (ranks - t)) % ranks, ranks))
-            return carry
-
-        lax.fori_loop(0, 2 - t // most, one, 0)
+            project(i % 2, near[i % 2], i // 2)
         return carry
 
-    project(me)
-    lax.fori_loop(1, most + 1, arrive, 0)
+    lax.fori_loop(2, most + 1, arrive, 0)
+    for piece in range(pieces):
+        project(0, rank_at((place + most) % ranks, ranks), piece)
 
     def exchange(source, target, r, send_sems, recv_sems):
         return [
@@ -756,6 +775,7 @@
                 [vmem((asks, blk), bf16)] * 2,
                 [vmem((asks, 128), f32)] * 2,
             ],
+            vmem((2, own, kv), bf16),
             pltpu.SMEM(lens.shape, lens.dtype),
             pltpu.SMEM(owner.shape, owner.dtype),
             pltpu.SMEM(ctx.shape, ctx.dtype),
@@ -853,7 +873,7 @@
 ):
     steps, rows_local, heads, width = dec_queries.shape
     ranks = lax.axis_size("head")
-    if heads % 16 or latent_rows.shape[0] % 128 or ranks % 2:
+    if heads % 16 or latent_rows.shape[0] % 128 or ranks % 2 or ranks < 8:
         return plain_on_device(
             latent_rows,
             pre_queries,

time: 54.4 us -> 56.6 us (1.040)
  Pallas kernels: 52.9 us -> 55.5 us
    pallas_call x1, Pallas kernels: 50.2 us -> 52.8 us  [serve_pallas(): pl.pallas_call(functools.partial(serve_kernel, lat=lat, ranks=ranks, head...]
where the time goes in v3:
time: 56.6 us; the launch traced here: 56.3 us
  Pallas kernels  55.5 us (98%)
  between operations  0.84 us (1%)
    pallas_call x1, Pallas kernels, serve_pallas(): pl.pallas_call(functools.partial(serve_kernel, lat=lat, ranks=ranks, head...  52.8 us
    pallas_call x1, Pallas kernels, project_pallas(): pl.pallas_call(functools.partial(project_kernel, heads=heads, lat=lat), o...  2.68 us

profile of v3, /device:TPU:0, one launch (start us, length us, event | category | flops | bytes accessed | tf_op | source)
XLA Modules:
  0.0 56.3 jit_solution(10475521918683346887)
XLA Ops:
  0.6 0.0 copy-start
  0.6 52.8 %shard_map.113 = (bf16[8,2,32,512]{3,2,1,0:T(8,128)(2,1)S(1)}, bf16[1024,2048]{1,0:T(8,128)(2,1)S(1)}) custom-call(s32[2,4]{1,0:T(2,128)} %lens_hbm.1, s32[2,4]{1,0:T(2,128)} %owner_hbm.1, s32[2]{0:T(128)} %ctx_hbm.1, bf16[2,2,576]{2,1,0:T(2,128)(2,1)} %new_hbm.1, bf16[576,128]{1,0:T(8,128)(2,1)} %bitcast.8, bf16[512,192]{1,0:T(8,128)(2,1)} %bitcast.7, ...), custom_call_target="tpu_custom_call" | custom-call | flops 30000001024 | bytes 25165824 | tf_op jit(solution)/shard_map/pallas_call | solution.py:732
  53.4 0.0 copy-done
  53.4 2.7 %shard_map.114 = (bf16[32,2048]{1,0:T(8,128)(2,1)}, bf16[1024,2048]{1,0:T(8,128)(2,1)}) custom-call(bf16[8,2,32,512]{3,2,1,0:T(8,128)(2,1)S(1)} %get-tuple-element.6.back_ref, bf16[512,2048]{1,0:T(8,128)(2,1)S(1)} %copy-done, bf16[1024,2048]{1,0:T(8,128)(2,1)S(1)} %get-tuple-element.7.part_ref), custom_call_target="tpu_custom_call" | custom-call | tf_op jit(solution)/shard_map/pallas_call | solution.py:846
Async XLA Ops:
  0.6 52.8 %copy-start = (bf16[512,2048]{1,0:T(8,128)(2,1)S(1)}, bf16[512,2048]{1,0:T(8,128)(2,1)}, u32[]{:S(2)}) copy-start(bf16[512,2048]{1,0:T(8,128)(2,1)} %vw_ref.1) | copy-start | bytes 6291460

commit v4 on v2

--- a/solution.py
+++ b/solution.py
@@ -247,13 +247,15 @@
 
 def attention(g, pair, qs, keys, tail, vals, hot, tri, part_ref, scores, weights, look, scale):
     span_len = tail.shape[0]
-    qb = tri.shape[0]
+    qb = 2 * tri.shape[0]
     blocks = span_len // qb
     order = [(0, p) for p in range(pair // 2)]
     order += [(i, p) for i in range(1, blocks) for p in range(pair)]
     order += [(0, p) for p in range(pair // 2, pair)]
     count = len(order)
     lengths = [min(i, look) + 1 for i, _ in order]
+    half = qb // 2
+    skips = [half if length == look + 1 else 0 for length in lengths]
     peaks = [None] * count
     tops = [None] * count
     sums = [None] * count
@@ -271,21 +273,41 @@
             [keys[g * pair + p, at : at + size, :], tail[at : at + size, :]], axis=1
         )
         s = jnp.dot(key, query, preferred_element_type=jnp.float32)
-        if size > qb:
-            scores[n % 4][: size - qb, :] = s[: size - qb]
-            peaks[n] = jnp.max(s[: size - qb].reshape((size - qb) // 8, 8, qb), axis=0)
-        last = s[size - qb :] + tri[...]
-        scores[n % 4][size - qb : size, :] = last
-        top = jnp.max(last.reshape(qb // 8, 8, qb), axis=0)
-        peaks[n] = top if peaks[n] is None else jnp.maximum(peaks[n], top)
+        left = [s[: size - qb, :half], s[size - qb : size - half, :half] + tri[...]]
+        right = [s[skips[n] : size - half, half:], s[size - half :, half:] + tri[...]]
+        row = 0
+        for piece in left:
+            if piece.shape[0]:
+                scores[n % 4][row : row + piece.shape[0], :half] = piece
+                row += piece.shape[0]
+        row = skips[n]
+        for piece in right:
+            scores[n % 4][row : row + piece.shape[0], half:] = piece
+            row += piece.shape[0]
+        both = []
+        for side in (left, right):
+            best = None
+            for piece in side:
+                if piece.shape[0]:
+                    top = jnp.max(piece.reshape(piece.shape[0] // 8, 8, half), axis=0)
+                    best = top if best is None else jnp.maximum(best, top)
+            both.append(best)
+        peaks[n] = both
 
     def soften(n, c):
         if c == 0:
-            tops[n] = jnp.max(peaks[n], axis=0, keepdims=True)
-        for k in range(0, qb, 32):
-            at = slice(c * qb + k, c * qb + k + 32)
-            w = jnp.exp2((scores[n % 4][at, :] - tops[n]) * scale)
-            weights[n % 4][at, :] = w.astype(jnp.bfloat16)
+            tops[n] = [jnp.max(peak, axis=0, keepdims=True) for peak in peaks[n]]
+        size = lengths[n] * qb
+        for side in range(2):
+            low, high = (0, size - half) if side == 0 else (skips[n], size)
+            lanes = slice(side * half, (side + 1) * half)
+            for k in range(c * qb, (c + 1) * qb, 64):
+                at = slice(k, k + 64)
+                if low <= k < high:
+                    w = jnp.exp2((scores[n % 4][at, lanes] - tops[n][side]) * scale)
+                    weights[n % 4][at, lanes] = w.astype(jnp.bfloat16)
+                else:
+                    weights[n % 4][at, lanes] = jnp.zeros((64, half), jnp.bfloat16)
 
     def mix(n, c):
         i, p = order[n]
@@ -733,7 +755,7 @@
             vmem((ranks, owned, block, kv), bf16),
             vmem((span_len, 128), bf16),
             vmem((marks, span_len), bf16),
-            vmem((qb, qb), f32),
+            vmem((qb // 2, qb // 2), f32),
             vmem(key_weight.shape, bf16),
             vmem(value_weight.shape, bf16),
             vmem((heads, width, span_len), bf16),

time: 54.4 us -> 54.4 us (level)
  no operation moved by 1% of the time
where the time goes in v4:
time: 54.4 us; the launch traced here: 54.3 us
  Pallas kernels  53.4 us (98%)
  between operations  0.82 us (2%)
    pallas_call x1, Pallas kernels, serve_pallas(): pl.pallas_call(functools.partial(serve_kernel, lat=lat, ranks=ranks, head...  50.8 us
    pallas_call x1, Pallas kernels, project_pallas(): pl.pallas_call(functools.partial(project_kernel, heads=heads, lat=lat), o...  2.68 us

profile of v4, /device:TPU:0, one launch (start us, length us, event | category | flops | bytes accessed | tf_op | source)
XLA Modules:
  0.0 54.3 jit_solution(10022967457851629733)
XLA Ops:
  0.6 0.0 copy-start
  0.6 50.8 %shard_map.113 = (bf16[8,2,32,512]{3,2,1,0:T(8,128)(2,1)S(1)}, bf16[1024,2048]{1,0:T(8,128)(2,1)S(1)}) custom-call(s32[2,4]{1,0:T(2,128)} %lens_hbm.1, s32[2,4]{1,0:T(2,128)} %owner_hbm.1, s32[2]{0:T(128)} %ctx_hbm.1, bf16[2,2,576]{2,1,0:T(2,128)(2,1)} %new_hbm.1, bf16[576,128]{1,0:T(8,128)(2,1)} %bitcast.8, bf16[512,192]{1,0:T(8,128)(2,1)} %bitcast.7, ...), custom_call_target="tpu_custom_call" | custom-call | flops 30000001024 | bytes 25165824 | tf_op jit(solution)/shard_map/pallas_call | solution.py:735
  51.4 0.0 copy-done
  51.4 2.7 %shard_map.114 = (bf16[32,2048]{1,0:T(8,128)(2,1)}, bf16[1024,2048]{1,0:T(8,128)(2,1)}) custom-call(bf16[8,2,32,512]{3,2,1,0:T(8,128)(2,1)S(1)} %get-tuple-element.6.back_ref, bf16[512,2048]{1,0:T(8,128)(2,1)S(1)} %copy-done, bf16[1024,2048]{1,0:T(8,128)(2,1)S(1)} %get-tuple-element.7.part_ref), custom_call_target="tpu_custom_call" | custom-call | tf_op jit(solution)/shard_map/pallas_call | solution.py:848
Async XLA Ops:
  0.6 50.8 %copy-start = (bf16[512,2048]{1,0:T(8,128)(2,1)S(1)}, bf16[512,2048]{1,0:T(8,128)(2,1)}, u32[]{:S(2)}) copy-start(bf16[512,2048]{1,0:T(8,128)(2,1)} %vw_ref.1) | copy-start | bytes 6291460

commit v5 on v4

--- a/solution.py
+++ b/solution.py
@@ -592,9 +592,6 @@
     ]
     for load in smalls + loads:
         load.start()
-    for small in smalls:
-        small.wait()
-    start_marks(span_ends(lens_ref, batch_rank), tail, vals, hot, tri)
     pl.semaphore_wait(barrier, ranks)
 
     quarter = shard_hbm.shape[0] // 4
@@ -604,8 +601,9 @@
         back_by = t - 1 if way == 0 else ranks - t + 1
         origin = rank_at((place + ranks - back_by) % ranks, ranks)
         rows = pl.ds(part * quarter, quarter)
+        begins = isinstance(t, int) and t == 1
         return pltpu.make_async_remote_copy(
-            src_ref=spans_ref.at[origin, rows],
+            src_ref=shard_hbm.at[rows] if begins else spans_ref.at[origin, rows],
             dst_ref=spans_ref.at[origin, rows],
             send_sem=ring_send.at[way, part, t - 1],
             recv_sem=ring_recv.at[way, part, t - 1],
@@ -617,38 +615,16 @@
         return most if way == part // 2 else most - 1
 
     streams = [(0, 0), (1, 2), (0, 1), (1, 3), (0, 2), (1, 0), (0, 3), (1, 1)]
-    loads[0].wait()
     for way, part in streams:
         hop(way, part, 1).start()
+    for small in smalls:
+        small.wait()
+    start_marks(span_ends(lens_ref, batch_rank), tail, vals, hot, tri)
+    loads[0].wait()
     loads[1].wait()
     loads[2].wait()
     absorb_into(dq, kw, sent, flat, wide, heads, lat)
     loads[3].wait()
-
-    def project(origin):
-        project_shard(origin, spans_ref, kw, vw, keys, vals, tail, lat, heads)
-
-    def arrive(t, carry):
-        for way, part in streams:
-            if hops(way, part) == most:
-                hop(way, part, t).wait_recv()
-                pl.when(t < most)(lambda: hop(way, part, t + 1).start())
-            else:
-
-                @pl.when(t < most)
-                def _():
-                    hop(way, part, t).wait_recv()
-                    pl.when(t < most - 1)(lambda: hop(way, part, t + 1).start())
-
-        def one(side, carry):
-            project(rank_at((place + side * t + (1 - side) * (ranks - t)) % ranks, ranks))
-            return carry
-
-        lax.fori_loop(0, 2 - t // most, one, 0)
-        return carry
-
-    project(me)
-    lax.fori_loop(1, most + 1, arrive, 0)
 
     def exchange(source, target, r, send_sems, recv_sems):
         return [
@@ -665,6 +641,37 @@
 
     gives = [exchange(sent, got, r, give_sems, take_sems) for r in range(owned)]
     backs = [exchange(lo, back, r, back_send, back_recv) for r in range(owned)]
+    def project(origin):
+        project_shard(origin, spans_ref, kw, vw, keys, vals, tail, lat, heads)
+
+    def arrive(t, carry):
+        for way, part in streams:
+            if hops(way, part) == most:
+                hop(way, part, t).wait_recv()
+                pl.when(t < most)(lambda: hop(way, part, t + 1).start())
+            else:
+
+                @pl.when(t < most)
+                def _():
+                    hop(way, part, t).wait_recv()
+                    pl.when(t < most - 1)(lambda: hop(way, part, t + 1).start())
+
+        @pl.when(t == most - 1)
+        def _():
+            for copies in gives:
+                for copy in copies:
+                    copy.start()
+
+        def one(side, carry):
+            project(rank_at((place + side * t + (1 - side) * (ranks - t)) % ranks, ranks))
+            return carry
+
+        lax.fori_loop(0, 2 - t // most, one, 0)
+        return carry
+
+    project(me)
+    lax.fori_loop(1, most + 1, arrive, 0)
+
     swap = pltpu.make_async_remote_copy(
         src_ref=spans_ref.at[:ranks],
         dst_ref=spans_ref.at[ranks:],
@@ -673,9 +680,6 @@
         device_id={"batch": 1 - batch_rank},
         device_id_type=MESH,
     )
-    for copies in gives:
-        for copy in copies:
-            copy.start()
     swap.start()
     keep = pltpu.make_async_copy(sent.at[me], got.at[me], load_sems.at[5])
     keep.start()

time: 54.4 us -> 52.3 us (0.961)
  Pallas kernels: 53.4 us -> 51.3 us
    pallas_call x1, Pallas kernels: 50.8 us -> 48.6 us  [serve_pallas(): pl.pallas_call(functools.partial(serve_kernel, lat=lat, ranks=ranks, head...]
where the time goes in v5:
time: 52.3 us; the launch traced here: 52.1 us
  Pallas kernels  51.3 us (98%)
  between operations  0.82 us (2%)
    pallas_call x1, Pallas kernels, serve_pallas(): pl.pallas_call(functools.partial(serve_kernel, lat=lat, ranks=ranks, head...  48.6 us
    pallas_call x1, Pallas kernels, project_pallas(): pl.pallas_call(functools.partial(project_kernel, heads=heads, lat=lat), o...  2.68 us

profile of v5, /device:TPU:0, one launch (start us, length us, event | category | flops | bytes accessed | tf_op | source)
XLA Modules:
  0.0 52.1 jit_solution(17361791817635608312)
XLA Ops:
  0.6 0.0 copy-start
  0.6 48.6 %shard_map.113 = (bf16[8,2,32,512]{3,2,1,0:T(8,128)(2,1)S(1)}, bf16[1024,2048]{1,0:T(8,128)(2,1)S(1)}) custom-call(s32[2,4]{1,0:T(2,128)} %lens_hbm.1, s32[2,4]{1,0:T(2,128)} %owner_hbm.1, s32[2]{0:T(128)} %ctx_hbm.1, bf16[2,2,576]{2,1,0:T(2,128)(2,1)} %new_hbm.1, bf16[576,128]{1,0:T(8,128)(2,1)} %bitcast.8, bf16[512,192]{1,0:T(8,128)(2,1)} %bitcast.7, ...), custom_call_target="tpu_custom_call" | custom-call | flops 30000001024 | bytes 25165824 | tf_op jit(solution)/shard_map/pallas_call | solution.py:739
  49.3 0.0 copy-done
  49.3 2.7 %shard_map.114 = (bf16[32,2048]{1,0:T(8,128)(2,1)}, bf16[1024,2048]{1,0:T(8,128)(2,1)}) custom-call(bf16[8,2,32,512]{3,2,1,0:T(8,128)(2,1)S(1)} %get-tuple-element.6.back_ref, bf16[512,2048]{1,0:T(8,128)(2,1)S(1)} %copy-done, bf16[1024,2048]{1,0:T(8,128)(2,1)S(1)} %get-tuple-element.7.part_ref), custom_call_target="tpu_custom_call" | custom-call | tf_op jit(solution)/shard_map/pallas_call | solution.py:852
Async XLA Ops:
  0.6 48.7 %copy-start = (bf16[512,2048]{1,0:T(8,128)(2,1)S(1)}, bf16[512,2048]{1,0:T(8,128)(2,1)}, u32[]{:S(2)}) copy-start(bf16[512,2048]{1,0:T(8,128)(2,1)} %vw_ref.1) | copy-start | bytes 6291460

commit v6 on v5

--- a/solution.py
+++ b/solution.py
@@ -636,7 +636,7 @@
                 device_id={"head": (me + k) % ranks},
                 device_id_type=MESH,
             )
-            for k in range(1, ranks)
+            for k in sorted(range(1, ranks), key=lambda k: abs(k - ranks // 2))
         ]
 
     gives = [exchange(sent, got, r, give_sems, take_sems) for r in range(owned)]

time: 52.3 us -> 52 us (level)
  no operation moved by 1% of the time
where the time goes in v6:
time: 52 us; the launch traced here: 51.9 us
  Pallas kernels  51.1 us (98%)
  between operations  0.82 us (2%)
    pallas_call x1, Pallas kernels, serve_pallas(): pl.pallas_call(functools.partial(serve_kernel, lat=lat, ranks=ranks, head...  48.4 us
    pallas_call x1, Pallas kernels, project_pallas(): pl.pallas_call(functools.partial(project_kernel, heads=heads, lat=lat), o...  2.68 us

profile of v6, /device:TPU:0, one launch (start us, length us, event | category | flops | bytes accessed | tf_op | source)
XLA Modules:
  0.0 51.9 jit_solution(13396093903348840329)
XLA Ops:
  0.6 0.0 copy-start
  0.6 48.4 %shard_map.113 = (bf16[8,2,32,512]{3,2,1,0:T(8,128)(2,1)S(1)}, bf16[1024,2048]{1,0:T(8,128)(2,1)S(1)}) custom-call(s32[2,4]{1,0:T(2,128)} %lens_hbm.1, s32[2,4]{1,0:T(2,128)} %owner_hbm.1, s32[2]{0:T(128)} %ctx_hbm.1, bf16[2,2,576]{2,1,0:T(2,128)(2,1)} %new_hbm.1, bf16[576,128]{1,0:T(8,128)(2,1)} %bitcast.8, bf16[512,192]{1,0:T(8,128)(2,1)} %bitcast.7, ...), custom_call_target="tpu_custom_call" | custom-call | flops 30000001024 | bytes 25165824 | tf_op jit(solution)/shard_map/pallas_call | solution.py:739
  49.0 0.0 copy-done
  49.0 2.7 %shard_map.114 = (bf16[32,2048]{1,0:T(8,128)(2,1)}, bf16[1024,2048]{1,0:T(8,128)(2,1)}) custom-call(bf16[8,2,32,512]{3,2,1,0:T(8,128)(2,1)S(1)} %get-tuple-element.6.back_ref, bf16[512,2048]{1,0:T(8,128)(2,1)S(1)} %copy-done, bf16[1024,2048]{1,0:T(8,128)(2,1)S(1)} %get-tuple-element.7.part_ref), custom_call_target="tpu_custom_call" | custom-call | tf_op jit(solution)/shard_map/pallas_call | solution.py:852
Async XLA Ops:
  0.6 48.4 %copy-start = (bf16[512,2048]{1,0:T(8,128)(2,1)S(1)}, bf16[512,2048]{1,0:T(8,128)(2,1)}, u32[]{:S(2)}) copy-start(bf16[512,2048]{1,0:T(8,128)(2,1)} %vw_ref.1) | copy-start | bytes 6291460

commit v7 on v6

--- a/solution.py
+++ b/solution.py
@@ -810,40 +810,41 @@
     ranks, owned, block, _ = back_ref.shape
     steps = block // heads
     local = ranks * owned
-    shown = pltpu.make_async_copy(part_ref, whole_ref, sems.at[0])
-    shown.start()
-    for p in range(ranks):
-        for r in range(owned):
-            at = (p * owned + r) * block
-            for c in range(lat // 128):
-                wide[c, at : at + block] = back_ref[p, r, :, c * 128 : (c + 1) * 128].astype(
-                    jnp.float32
-                )
-
-    def some_heads(g, carry):
-        for p in range(4):
-            h = g * 4 + p
-            mine = jnp.concatenate(
-                [
-                    jnp.concatenate(
-                        [
-                            wide[c, pl.ds(s * heads + h, local, stride=block), :]
-                            for c in range(lat // 128)
-                        ],
-                        axis=1,
-                    )
-                    for s in range(steps)
-                ],
-                axis=0,
-            ).astype(jnp.bfloat16)
-            columns = pl.ds(pl.multiple_of(h * 128, 128), 128)
-            out_ref[:, columns] = jnp.dot(
-                mine, vw_ref[:, columns], preferred_element_type=jnp.float32
-            ).astype(jnp.bfloat16)
+    cut = part_ref.shape[0] // 4
+    shown = [
+        pltpu.make_async_copy(
+            part_ref.at[pl.ds(k * cut, cut)], whole_ref.at[pl.ds(k * cut, cut)], sems.at[k]
+        )
+        for k in range(4)
+    ]
+    for copy in shown:
+        copy.start()
+    rows = local * block
+    kept = steps * local
+
+    def gather(g, carry):
+        count = wide.shape[0] // 2
+        out = g * count + lax.broadcasted_iota(jnp.int32, (count, 1), 0)
+        head, rest = out // kept, out % kept
+        wanted = (rest % local) * block + (rest // local) * heads + head
+        source = lax.broadcasted_iota(jnp.int32, (count, rows), 1)
+        pick = jnp.where(source == wanted, 1.0, 0.0).astype(jnp.bfloat16)
+        wide[pl.ds(pl.multiple_of(g * count, count), count), :] = jnp.dot(
+            pick, back_ref[...].reshape(rows, lat), preferred_element_type=jnp.float32
+        ).astype(jnp.bfloat16)
         return carry
 
-    lax.fori_loop(0, heads // 4, some_heads, 0)
-    shown.wait()
+    lax.fori_loop(0, 2, gather, 0)
+    for h in range(0, heads, 2):
+        made = jnp.dot(
+            wide[h * kept : (h + 2) * kept, :],
+            vw_ref[:, h * 128 : (h + 2) * 128],
+            preferred_element_type=jnp.float32,
+        ).astype(jnp.bfloat16)
+        out_ref[:, h * 128 : (h + 1) * 128] = made[:kept, :128]
+        out_ref[:, (h + 1) * 128 : (h + 2) * 128] = made[kept:, 128:]
+    for copy in shown:
+        copy.wait()
 
 
 def project_pallas(back, value_weight, part, heads):
@@ -858,8 +859,8 @@
         in_specs=[VMEM_SPEC, VMEM_SPEC, VMEM_SPEC],
         out_specs=(VMEM_SPEC, HBM_SPEC),
         scratch_shapes=[
-            pltpu.VMEM((lat // 128, rows, 128), jnp.float32),
-            pltpu.SemaphoreType.DMA((1,)),
+            pltpu.VMEM((rows, lat), jnp.bfloat16),
+            pltpu.SemaphoreType.DMA((4,)),
         ],
         compiler_params=pltpu.CompilerParams(vmem_limit_bytes=8 << 20),
     )(back, value_weight, part)

time: 52 us -> 52.1 us (level)
  no operation moved by 1% of the time
where the time goes in v7:
time: 52.1 us; the launch traced here: 51.9 us
  Pallas kernels  51.1 us (98%)
  between operations  0.82 us (2%)
    pallas_call x1, Pallas kernels, serve_pallas(): pl.pallas_call(functools.partial(serve_kernel, lat=lat, ranks=ranks, head...  48.4 us
    pallas_call x1, Pallas kernels, project_pallas(): pl.pallas_call(functools.partial(project_kernel, heads=heads, lat=lat), o...  2.7 us

profile of v7, /device:TPU:0, one launch (start us, length us, event | category | flops | bytes accessed | tf_op | source)
XLA Modules:
  0.0 51.9 jit_solution(12638747302157534569)
XLA Ops:
  0.6 0.0 copy-start
  0.6 48.4 %shard_map.113 = (bf16[8,2,32,512]{3,2,1,0:T(8,128)(2,1)S(1)}, bf16[1024,2048]{1,0:T(8,128)(2,1)S(1)}) custom-call(s32[2,4]{1,0:T(2,128)} %lens_hbm.1, s32[2,4]{1,0:T(2,128)} %owner_hbm.1, s32[2]{0:T(128)} %ctx_hbm.1, bf16[2,2,576]{2,1,0:T(2,128)(2,1)} %new_hbm.1, bf16[576,128]{1,0:T(8,128)(2,1)} %bitcast.8, bf16[512,192]{1,0:T(8,128)(2,1)} %bitcast.7, ...), custom_call_target="tpu_custom_call" | custom-call | flops 30000001024 | bytes 25165824 | tf_op jit(solution)/shard_map/pallas_call | solution.py:739
  49.0 0.0 copy-done
  49.0 2.7 %shard_map.114 = (bf16[32,2048]{1,0:T(8,128)(2,1)}, bf16[1024,2048]{1,0:T(8,128)(2,1)}) custom-call(bf16[8,2,32,512]{3,2,1,0:T(8,128)(2,1)S(1)} %get-tuple-element.6.back_ref, bf16[512,2048]{1,0:T(8,128)(2,1)S(1)} %copy-done, bf16[1024,2048]{1,0:T(8,128)(2,1)S(1)} %get-tuple-element.7.part_ref), custom_call_target="tpu_custom_call" | custom-call | tf_op jit(solution)/shard_map/pallas_call | solution.py:853
Async XLA Ops:
  0.6 48.4 %copy-start = (bf16[512,2048]{1,0:T(8,128)(2,1)S(1)}, bf16[512,2048]{1,0:T(8,128)(2,1)}, u32[]{:S(2)}) copy-start(bf16[512,2048]{1,0:T(8,128)(2,1)} %vw_ref.1) | copy-start | bytes 6291460
